TPU v7x, 32 devices: a whole 2x2x4 slice. The times are simulated.
32 devices in a mesh: groups: 2 (over y), ctx: 4 (over z), head: 2 (over x), rep: 2 (over core).
Axes of the slice: x: 2, y: 2, z: 4, core: 2. Of those that a mesh axis runs over, the one named last changes fastest.
Arguments:
- kv_cache: bfloat16 [4, 96, 128, 576], P(('groups', 'rep'), 'ctx'), parts along dimension 0, may hold values from -10 to 10
- queries: bfloat16 [4, 4, 128, 576], P(('groups', 'rep'), None, 'head'), parts along dimension 0, may hold values from -45 to 45
- new_latent: bfloat16 [4, 4, 576], P(('groups', 'rep')), parts along dimension 0, may hold values from -6 to 6
- page_counts: int32 [4, 4], P(('groups', 'rep')), parts along dimension 0, may hold values from 1 to 36, 72 in all within a row
- page_tails: int32 [4, 4], P(('groups', 'rep')), parts along dimension 0, may hold values from 1 to 128
- page_slots: int32 [4, 96], P(('groups', 'rep')), parts along dimension 0, may hold values from 0 to 95, each once within a row
Outputs:
- attended: bfloat16 [4, 4, 128, 512], P(('groups', 'rep'), None, 'head'), parts along dimension 0
There are 2 independent parts, one for each index of `groups`. A program takes and returns all parts, laid end to end along the dimension named above; each array names one. Nothing has to cross between parts.
Inputs may be any that keep to these rules, and one draw needn't show every extreme that they name: `page_counts`: the 4 counts of a half sum to 72, and the largest is exactly 36. `page_slots`: each half's row holds every slot once; only its first 72 entries are pages in use.
All inputs are finite; a program needn't handle non-finite values.
Results may differ from a plain program's by a relative error of at most 0.0033.
Values sent between devices are 32-bit elements; how exact they have to be, the bound alone decides.
A program may use at most 64 MiB of HBM per device.

v0:
```python
import jax
import jax.numpy as jnp
from jax import lax
from jax.sharding import PartitionSpec as P

LATENT = 512


score_scale = 192.0 ** (-0.5)
neg_large = -1e30


def from_behind(shard, axis, by):
    size = lax.axis_size(axis)
    return lax.ppermute(shard, axis, [(i, (i + by) % size) for i in range(size)])


def page_layout(page_counts, page_tails, page_slots, pages_local, page_width):
    ctx_place = lax.axis_index("ctx")
    counts = page_counts[0]
    slot_ids = ctx_place * pages_local + jnp.arange(pages_local, dtype=jnp.int32)
    pack_rank = jnp.arange(page_slots.shape[1], dtype=jnp.int32)
    matches = page_slots[0][:, None] == slot_ids[None, :]
    page_rank = jnp.sum(jnp.where(matches, pack_rank[:, None], 0), axis=0)
    ends = jnp.cumsum(counts)
    starts = ends - counts
    page_live = page_rank < ends[-1]
    sequence_of = jnp.sum((ends[None, :] <= page_rank[:, None]).astype(jnp.int32), axis=1)
    sequence_of = jnp.minimum(sequence_of, counts.shape[0] - 1)
    page_number = page_rank - jnp.take(starts, sequence_of)
    lengths = (counts - 1) * page_width + page_tails[0]
    limit = jnp.take(lengths, sequence_of) - page_number * page_width
    token_place = jnp.arange(page_width, dtype=jnp.int32)
    token_valid = page_live[:, None] & (token_place[None, :] < limit[:, None])
    return (sequence_of, page_live, token_valid)


def page_partials(query_pages, cache_pages, token_valid):
    scores = (
        jnp.einsum("phc,ptc->pht", query_pages, cache_pages, preferred_element_type=jnp.float32)
        * score_scale
    )
    masked = jnp.where(token_valid[:, None, :], scores, neg_large)
    page_max = jnp.max(masked, axis=2)
    weights = jnp.where(
        token_valid[:, None, :], jnp.exp(masked - page_max[:, :, None]), 0.0
    ).astype(jnp.bfloat16)
    page_sum = jnp.sum(weights.astype(jnp.float32), axis=2)
    page_acc = jnp.einsum(
        "pht,ptc->phc", weights, cache_pages[:, :, :LATENT], preferred_element_type=jnp.float32
    )
    return (page_max, page_sum, page_acc)


def fold_pages(partials, owner, rows):
    page_max, page_sum, page_acc = partials
    member = owner[:, None] == jnp.arange(rows, dtype=jnp.int32)[None, :]
    row_max = jnp.max(jnp.where(member[:, :, None], page_max[:, None, :], neg_large), axis=0)
    owner_max = jnp.take(row_max, jnp.clip(owner, 0, rows - 1), axis=0)
    factor = jnp.where((owner >= 0)[:, None], jnp.exp(page_max - owner_max), 0.0)
    onehot = member.astype(jnp.float32)
    row_sum = jnp.einsum("ps,ph->sh", onehot, factor * page_sum, precision=lax.Precision.HIGHEST)
    row_acc = jnp.einsum(
        "ps,phc->shc", onehot, factor[:, :, None] * page_acc, precision=lax.Precision.HIGHEST
    )
    return (row_max, row_sum, row_acc)


def merge_states(first, second):
    top = jnp.maximum(first[0], second[0])
    keep_first = jnp.exp(first[0] - top)
    keep_second = jnp.exp(second[0] - top)
    return (
        top,
        first[1] * keep_first + second[1] * keep_second,
        first[2] * keep_first[..., None] + second[2] * keep_second[..., None],
    )


def local(kv_cache, queries, new_latent, page_counts, page_tails, page_slots):
    pages_local = kv_cache.shape[1]
    page_width = kv_cache.shape[2]
    cache_pages = kv_cache[0]
    sequence_of, page_live, token_valid = page_layout(
        page_counts, page_tails, page_slots, pages_local, page_width
    )
    query_block = queries[0]
    batch_rows = query_block.shape[0]
    cycle_size = lax.axis_size("ctx")
    query_pages = jnp.take(query_block, sequence_of, axis=0)
    partials = page_partials(query_pages, cache_pages, token_valid)
    owner = jnp.where(page_live, sequence_of, -1)
    local_max, local_sum, local_acc = fold_pages(partials, owner, batch_rows)

    def visit(hop_index, carried):
        travel, gathered = carried
        arrived = from_behind((travel[0], travel[1], travel[2]), "ctx", 1)
        merged = merge_states(gathered, arrived)
        return (arrived, merged)

    local_state = (local_max, local_sum, local_acc)
    finished = lax.fori_loop(0, cycle_size - 1, visit, (local_state, local_state))
    row_max, row_sum, row_acc = finished[1]
    own_row = new_latent[0].astype(jnp.float32)
    own_score = (
        jnp.einsum("shc,sc->sh", query_block, new_latent[0], preferred_element_type=jnp.float32)
        * score_scale
    )
    top = jnp.maximum(row_max, own_score)
    keep_old = jnp.exp(row_max - top)
    own_factor = jnp.exp(own_score - top)
    numer = row_acc * keep_old[:, :, None] + own_factor[:, :, None] * own_row[:, None, :LATENT]
    denom = row_sum * keep_old + own_factor
    return (numer / denom[:, :, None]).astype(jnp.bfloat16)[None]


def solution(mesh):
    in_specs = (
        P(("groups", "rep"), "ctx", None, None),
        P(("groups", "rep"), None, "head", None),
        P(("groups", "rep"), None, None),
        P(("groups", "rep"), None),
        P(("groups", "rep"), None),
        P(("groups", "rep"), None),
    )
    out_specs = P(("groups", "rep"), None, "head", None)
    return jax.shard_map(local, mesh=mesh, in_specs=in_specs, out_specs=out_specs, check_vma=False)
```

profile of v0, /device:TPU:0, one launch (start us, length us, event | category | flops | bytes accessed | tf_op | source)
XLA Modules:
  0.0 70.1 jit_solution(13343445531454991762)
XLA Ops:
  0.0 0.0 copy-start
  0.0 1.0 %copy-done = bf16[1,4,64,576]{3,2,1,0:T(8,128)(2,1)S(1)} copy-done((bf16[1,4,64,576]{3,2,1,0:T(8,128)(2,1)S(1)}, bf16[1,4,64,576]{3,2,1,0:T(8,128)(2,1)}, u32[]{:S(2)}) %copy-start) | copy-done | bytes 294936
  1.0 0.8 %select_reduce_fusion.1 = s32[24]{0:T(128)S(1)} fusion(s32[96]{0:T(128)} %bitcast.63, s32[24]{0:T(128)S(1)} %iota_add_fusion), kind=kLoop, calls=%fused_computation.26 | loop fusion | flops 6888 | bytes 576 | tf_op jit(solution)/shard_map/reduce_sum | solution.py:24
  1.8 0.8 %reduce-window.4 = s32[4,1]{0,1:T(1,128)S(1)} reduce-window(s32[4,1]{0,1:T(1,128)} %bitcast.61, s32[]{:T(128)} %copy.43), window={size=4x1 pad=3_0x0_0}, to_apply=%region_1.2 | reduce-window | flops 12 | bytes 36 | tf_op jit(solution)/shard_map/reduce-window
  2.6 0.1 convert_reduce_fusion.1
  2.7 0.7 slice.13
  3.4 0.7 broadcast_compare_fusion
  4.1 0.9 %gather_fusion = bf16[24,64,576]{2,1,0:T(8,128)(2,1)S(1)} fusion(bf16[4,64,576]{2,1,0:T(8,128)(2,1)S(1)} %bitcast.56, s32[1024]{0:T(1024)S(1)} %get-tuple-element.106), kind=kCustom, calls=%fused_computation | custom fusion | bytes 3539040 | tf_op jit(solution)/shard_map/jit(_take)/gather | solution.py:90
  5.1 0.0 copy-done.3
  5.1 0.0 copy-done.4
  5.1 0.7 fusion.37
  5.8 5.0 %fusion.24 = s32[24]{0:T(128)S(1)} fusion(s32[24]{0:T(128)S(1)} %select_reduce_fusion.1, s32[]{:T(128)} %bitcast.13, s32[]{:T(128)} %bitcast.12, s32[]{:T(128)} %bitcast.11, s32[]{:T(128)} %bitcast.10, s32[]{:T(128)} %bitcast.9, s32[]{:T(128)} %bitcast.8, s32[]{:T(128)} %bitcast.7, s32[]{:T(128)} %bitcast.6, s32[24]{0:T(128)S(1)} %convert_reduce_fusion.1), kind=kLoop, calls=%fused_computation.55 | loop fusion | flops 504 | bytes 320 | tf_op jit(solution)/shard_map/sub | solution.py:32
  10.8 0.1 fusion.17
  10.9 3.1 %fusion.39 = (f32[24,64]{1,0:T(8,128)S(1)}, f32[24,64,128]{2,1,0:T(8,128)S(1)}) fusion(bf16[1,24,128,576]{2,3,1,0:T(8,128)(2,1)} %param.10, bf16[24,64,576]{2,1,0:T(8,128)(2,1)S(1)} %gather_fusion, pred[24]{0:T(512)(128)(4,1)S(1)} %get-tuple-element.88, pred[24,128]{1,0:T(8,128)(4,1)S(1)} %fusion.17), kind=kOutput, calls=%fused_computation.76 | convolution fusion | flops 227965440 | bytes 6104088 | tf_op jit(solution)/shard_map/phc,ptc->pht/dot_general | solution.py:40
  13.9 0.1 select_reduce_fusion
  14.0 0.6 gather_fusion.1
  14.6 0.1 exponential_select_fusion
  14.7 0.5 convert_reduce_fusion
  15.2 0.1 fusion.15
  15.4 3.4 %fusion = f32[24,64,512]{2,1,0:T(8,128)S(1)} fusion(bf16[24,128,576]{1,2,0:T(8,128)(2,1)} %bitcast.57, f32[24,64,128]{2,1,0:T(8,128)} %copy-done.1, f32[24,64]{1,0:T(8,128)S(1)} %get-tuple-element.99, pred[24,128]{1,0:T(8,128)(4,1)S(1)} %fusion.17), kind=kOutput, calls=%fused_computation.6 | convolution fusion | flops 201916416 | bytes 7087104 | tf_op jit(solution)/shard_map/pht,ptc->phc/dot_general | solution.py:49
  18.8 0.1 copy.11
  18.9 2.7 %fusion.2 = f32[4,64,512]{2,0,1:T(4,128)S(1)} fusion(f32[24,64,512]{2,1,0:T(8,128)S(1)} %fusion, f32[24,64]{0,1:T(8,128)S(1)} %copy.11, s32[24]{0:T(128)S(1)} %get-tuple-element.84), kind=kOutput, calls=%fused_computation.9 | convolution fusion | flops 38535264 | bytes 3676256 | tf_op jit(solution)/shard_map/ps,phc->shc/dot_general | solution.py:63
  21.6 0.2 copy.12
  21.8 0.0 copy-start.2
  21.8 47.1 %while.20 = (s32[]{:T(128)}, f32[4,64]{1,0:T(4,128)S(1)}, f32[4,64]{1,0:T(4,128)S(1)}, f32[4,64,512]{2,1,0:T(8,128)S(1)}, f32[4,64]{1,0:T(4,128)S(1)}, /*index=5...) while((s32[]{:T(128)}, f32[4,64]{1,0:T(4,128)S(1)}, f32[4,64]{1,0:T(4,128)S(1)}, ...), condition=%wide.region_7.9_spmd, body=%wide.region_6.8_spmd.sunk | while | flops 394754 | bytes 4741325 | solution.py:102
  21.8 3.1 %collective-permute-start.2 = (f32[4,64,512]{2,1,0:T(8,128)S(1)}, f32[4,64,512]{2,1,0:T(8,128)S(1)}, u32[]{:S(2)}, u32[]{:S(2)}) collective-permute-start(f32[4,64,512]{2,1,0:T(8,128)S(1)} %get-tuple-element.169), channel_id=1, source_target_pairs={{0,4},{4,8},{8,12},{12,0},{1,5},{5,9},{9,13},{13,1},{2,6},{6,10},{... | collective-permute-start | bytes 1572872 | tf_op jit(solution)/shard_map/while/body/eval_jaxpr/ppermute | solution.py:15
  24.9 1.6 %collective-permute-start = (f32[4,64]{1,0:T(4,128)S(1)}, f32[4,64]{1,0:T(4,128)S(1)}, u32[]{:S(2)}, u32[]{:S(2)}) collective-permute-start(f32[4,64]{1,0:T(4,128)S(1)} %get-tuple-element.167), channel_id=1, source_target_pairs={{0,4},{4,8},{8,12},{12,0},{1,5},{5,9},{9,13},{13,1},{2,6},{6,10},{... | collective-permute-start | bytes 3080 | tf_op jit(solution)/shard_map/while/body/eval_jaxpr/ppermute | solution.py:15
  26.5 1.6 %collective-permute-start.1 = (f32[4,64]{1,0:T(4,128)S(1)}, f32[4,64]{1,0:T(4,128)S(1)}, u32[]{:S(2)}, u32[]{:S(2)}) collective-permute-start(f32[4,64]{1,0:T(4,128)S(1)} %get-tuple-element.168), channel_id=1, source_target_pairs={{0,4},{4,8},{8,12},{12,0},{1,5},{5,9},{9,13},{13,1},{2,6},{6,10},{... | collective-permute-start | bytes 3080 | tf_op jit(solution)/shard_map/while/body/eval_jaxpr/ppermute | solution.py:15
  28.1 10.9 %collective-permute-done = f32[4,64]{1,0:T(4,128)S(1)} collective-permute-done((f32[4,64]{1,0:T(4,128)S(1)}, f32[4,64]{1,0:T(4,128)S(1)}, u32[]{:S(2)}, u32[]{:S(2)}) %collective-permute-start) | collective-permute-done | bytes 1056 | tf_op jit(solution)/shard_map/while/body/eval_jaxpr/ppermute | solution.py:15
  38.9 0.0 collective-permute-done.1
  39.0 0.0 collective-permute-done.2
  39.0 0.2 multiply_add_fusion.6
  39.2 0.1 collective-permute-start.2
  39.3 1.3 %collective-permute-start = (f32[4,64]{1,0:T(4,128)S(1)}, f32[4,64]{1,0:T(4,128)S(1)}, u32[]{:S(2)}, u32[]{:S(2)}) collective-permute-start(f32[4,64]{1,0:T(4,128)S(1)} %get-tuple-element.167), channel_id=1, source_target_pairs={{0,4},{4,8},{8,12},{12,0},{1,5},{5,9},{9,13},{13,1},{2,6},{6,10},{... | collective-permute-start | bytes 3080 | tf_op jit(solution)/shard_map/while/body/eval_jaxpr/ppermute | solution.py:15
  40.6 1.6 %collective-permute-start.1 = (f32[4,64]{1,0:T(4,128)S(1)}, f32[4,64]{1,0:T(4,128)S(1)}, u32[]{:S(2)}, u32[]{:S(2)}) collective-permute-start(f32[4,64]{1,0:T(4,128)S(1)} %get-tuple-element.168), channel_id=1, source_target_pairs={{0,4},{4,8},{8,12},{12,0},{1,5},{5,9},{9,13},{13,1},{2,6},{6,10},{... | collective-permute-start | bytes 3080 | tf_op jit(solution)/shard_map/while/body/eval_jaxpr/ppermute | solution.py:15
  42.1 12.1 %collective-permute-done = f32[4,64]{1,0:T(4,128)S(1)} collective-permute-done((f32[4,64]{1,0:T(4,128)S(1)}, f32[4,64]{1,0:T(4,128)S(1)}, u32[]{:S(2)}, u32[]{:S(2)}) %collective-permute-start) | collective-permute-done | bytes 1056 | tf_op jit(solution)/shard_map/while/body/eval_jaxpr/ppermute | solution.py:15
  54.2 0.0 collective-permute-done.1
  54.3 0.0 collective-permute-done.2
  54.3 0.2 multiply_add_fusion.6
  54.5 0.1 collective-permute-start.2
  54.6 0.1 collective-permute-start
  54.6 0.7 %collective-permute-start.1 = (f32[4,64]{1,0:T(4,128)S(1)}, f32[4,64]{1,0:T(4,128)S(1)}, u32[]{:S(2)}, u32[]{:S(2)}) collective-permute-start(f32[4,64]{1,0:T(4,128)S(1)} %get-tuple-element.168), channel_id=1, source_target_pairs={{0,4},{4,8},{8,12},{12,0},{1,5},{5,9},{9,13},{13,1},{2,6},{6,10},{... | collective-permute-start | bytes 3080 | tf_op jit(solution)/shard_map/while/body/eval_jaxpr/ppermute | solution.py:15
  55.4 13.3 %collective-permute-done = f32[4,64]{1,0:T(4,128)S(1)} collective-permute-done((f32[4,64]{1,0:T(4,128)S(1)}, f32[4,64]{1,0:T(4,128)S(1)}, u32[]{:S(2)}, u32[]{:S(2)}) %collective-permute-start) | collective-permute-done | bytes 1056 | tf_op jit(solution)/shard_map/while/body/eval_jaxpr/ppermute | solution.py:15
  68.7 0.0 collective-permute-done.1
  68.7 0.0 collective-permute-done.2
  68.8 0.2 multiply_add_fusion.6
  69.0 0.2 fusion.18
  69.2 0.9 %fusion.14 = bf16[1,4,64,512]{3,2,1,0:T(8,128)(2,1)} fusion(f32[4,64]{1,0:T(4,128)S(1)} %get-tuple-element.80, f32[4,512]{1,0:T(4,128)S(1)} %slice_convert_fusion, f32[4,64]{1,0:T(4,128)S(1)} %get-tuple-element.82, f32[4,64,512]{2,1,0:T(8,128)S(1)} %get-tuple-element.45, f32[4,64]{1,0:T(4,128)S(1)} %get-tuple-element.81), kind=kLoop, calls=%fused_computation.20 | loop fusion | flops 655360 | bytes 797696 | tf_op jit(solution)/shard_map/broadcast_in_dim | solution.py:114
  (28 shorter events, 0.3 us)
Async XLA Ops:
  0.0 1.0 %copy-start = (bf16[1,4,64,576]{3,2,1,0:T(8,128)(2,1)S(1)}, bf16[1,4,64,576]{3,2,1,0:T(8,128)(2,1)}, u32[]{:S(2)}) copy-start(bf16[1,4,64,576]{3,2,1,0:T(8,128)(2,1)} %param.11) | copy-start | bytes 884740
  0.0 5.1 %copy-start.3 = (s32[1,4]{1,0:T(1,128)S(1)}, s32[1,4]{1,0:T(1,128)}, u32[]{:S(2)}) copy-start(s32[1,4]{1,0:T(1,128)} %param.13) | copy-start | bytes 52
  0.0 5.1 %copy-start.4 = (s32[1,4]{1,0:T(1,128)S(1)}, s32[1,4]{1,0:T(1,128)}, u32[]{:S(2)}) copy-start(s32[1,4]{1,0:T(1,128)} %param.14) | copy-start | bytes 52
  13.9 1.4 %copy-start.1 = (f32[24,64,128]{2,1,0:T(8,128)}, f32[24,64,128]{2,1,0:T(8,128)S(1)}, u32[]{:S(2)}) copy-start(f32[24,64,128]{2,1,0:T(8,128)S(1)} %get-tuple-element.100) | copy-start | bytes 2359300
  21.8 47.1 %copy-start.2 = (bf16[1,4,576]{2,1,0:T(4,128)(2,1)S(1)}, bf16[1,4,576]{2,1,0:T(4,128)(2,1)}, u32[]{:S(2)}) copy-start(bf16[1,4,576]{2,1,0:T(4,128)(2,1)} %param.12) | copy-start | bytes 13828
  21.8 17.2 %collective-permute-start.2 = (f32[4,64,512]{2,1,0:T(8,128)S(1)}, f32[4,64,512]{2,1,0:T(8,128)S(1)}, u32[]{:S(2)}, u32[]{:S(2)}) collective-permute-start(f32[4,64,512]{2,1,0:T(8,128)S(1)} %get-tuple-element.169), channel_id=1, source_target_pairs={{0,4},{4,8},{8,12},{12,0},{1,5},{5,9},{9,13},{13,1},{2,6},{6,10},{... | collective-permute-start | bytes 1572872 | tf_op jit(solution)/shard_map/while/body/eval_jaxpr/ppermute | solution.py:15
  24.9 14.0 %collective-permute-start = (f32[4,64]{1,0:T(4,128)S(1)}, f32[4,64]{1,0:T(4,128)S(1)}, u32[]{:S(2)}, u32[]{:S(2)}) collective-permute-start(f32[4,64]{1,0:T(4,128)S(1)} %get-tuple-element.167), channel_id=1, source_target_pairs={{0,4},{4,8},{8,12},{12,0},{1,5},{5,9},{9,13},{13,1},{2,6},{6,10},{... | collective-permute-start | bytes 3080 | tf_op jit(solution)/shard_map/while/body/eval_jaxpr/ppermute | solution.py:15
  26.5 12.5 %collective-permute-start.1 = (f32[4,64]{1,0:T(4,128)S(1)}, f32[4,64]{1,0:T(4,128)S(1)}, u32[]{:S(2)}, u32[]{:S(2)}) collective-permute-start(f32[4,64]{1,0:T(4,128)S(1)} %get-tuple-element.168), channel_id=1, source_target_pairs={{0,4},{4,8},{8,12},{12,0},{1,5},{5,9},{9,13},{13,1},{2,6},{6,10},{... | collective-permute-start | bytes 3080 | tf_op jit(solution)/shard_map/while/body/eval_jaxpr/ppermute | solution.py:15
  39.2 15.1 %collective-permute-start.2 = (f32[4,64,512]{2,1,0:T(8,128)S(1)}, f32[4,64,512]{2,1,0:T(8,128)S(1)}, u32[]{:S(2)}, u32[]{:S(2)}) collective-permute-start(f32[4,64,512]{2,1,0:T(8,128)S(1)} %get-tuple-element.169), channel_id=1, source_target_pairs={{0,4},{4,8},{8,12},{12,0},{1,5},{5,9},{9,13},{13,1},{2,6},{6,10},{... | collective-permute-start | bytes 1572872 | tf_op jit(solution)/shard_map/while/body/eval_jaxpr/ppermute | solution.py:15
  39.3 14.9 %collective-permute-start = (f32[4,64]{1,0:T(4,128)S(1)}, f32[4,64]{1,0:T(4,128)S(1)}, u32[]{:S(2)}, u32[]{:S(2)}) collective-permute-start(f32[4,64]{1,0:T(4,128)S(1)} %get-tuple-element.167), channel_id=1, source_target_pairs={{0,4},{4,8},{8,12},{12,0},{1,5},{5,9},{9,13},{13,1},{2,6},{6,10},{... | collective-permute-start | bytes 3080 | tf_op jit(solution)/shard_map/while/body/eval_jaxpr/ppermute | solution.py:15
  40.6 13.7 %collective-permute-start.1 = (f32[4,64]{1,0:T(4,128)S(1)}, f32[4,64]{1,0:T(4,128)S(1)}, u32[]{:S(2)}, u32[]{:S(2)}) collective-permute-start(f32[4,64]{1,0:T(4,128)S(1)} %get-tuple-element.168), channel_id=1, source_target_pairs={{0,4},{4,8},{8,12},{12,0},{1,5},{5,9},{9,13},{13,1},{2,6},{6,10},{... | collective-permute-start | bytes 3080 | tf_op jit(solution)/shard_map/while/body/eval_jaxpr/ppermute | solution.py:15
  54.5 14.2 %collective-permute-start.2 = (f32[4,64,512]{2,1,0:T(8,128)S(1)}, f32[4,64,512]{2,1,0:T(8,128)S(1)}, u32[]{:S(2)}, u32[]{:S(2)}) collective-permute-start(f32[4,64,512]{2,1,0:T(8,128)S(1)} %get-tuple-element.169), channel_id=1, source_target_pairs={{0,4},{4,8},{8,12},{12,0},{1,5},{5,9},{9,13},{13,1},{2,6},{6,10},{... | collective-permute-start | bytes 1572872 | tf_op jit(solution)/shard_map/while/body/eval_jaxpr/ppermute | solution.py:15
  54.6 14.1 %collective-permute-start = (f32[4,64]{1,0:T(4,128)S(1)}, f32[4,64]{1,0:T(4,128)S(1)}, u32[]{:S(2)}, u32[]{:S(2)}) collective-permute-start(f32[4,64]{1,0:T(4,128)S(1)} %get-tuple-element.167), channel_id=1, source_target_pairs={{0,4},{4,8},{8,12},{12,0},{1,5},{5,9},{9,13},{13,1},{2,6},{6,10},{... | collective-permute-start | bytes 3080 | tf_op jit(solution)/shard_map/while/body/eval_jaxpr/ppermute | solution.py:15
  54.6 14.0 %collective-permute-start.1 = (f32[4,64]{1,0:T(4,128)S(1)}, f32[4,64]{1,0:T(4,128)S(1)}, u32[]{:S(2)}, u32[]{:S(2)}) collective-permute-start(f32[4,64]{1,0:T(4,128)S(1)} %get-tuple-element.168), channel_id=1, source_target_pairs={{0,4},{4,8},{8,12},{12,0},{1,5},{5,9},{9,13},{13,1},{2,6},{6,10},{... | collective-permute-start | bytes 3080 | tf_op jit(solution)/shard_map/while/body/eval_jaxpr/ppermute | solution.py:15
where the time goes:
time: 70.3 us; the launch traced here: 70.1 us
  waiting for transfers between devices  36.3 us (52%)
  starting transfers between devices  10 us (14%)
  other arithmetic  9.72 us (14%)
  matrix products  9.49 us (13%)
  local copies, waits for them, and re-layouts  4.24 us (6%)
    ppermute x9, waiting for transfers between devices, from_behind(): lax.ppermute(shard, axis, [(i, (i + by) % size) for i in range(size)])  36.3 us
    ppermute x9, starting transfers between devices, from_behind(): lax.ppermute(shard, axis, [(i, (i + by) % size) for i in range(size)])  10 us
    sub x1, other arithmetic, page_layout(): limit = jnp.take(lengths, sequence_of) - page_number * page_width  4.99 us
    dot_general x1, matrix products, page_partials(): jnp.einsum('pht,ptc->phc', weights, cache_pages[:, :, :LATENT], preferred...  3.42 us
    dot_general x1, matrix products, page_partials(): jnp.einsum('phc,ptc->pht', query_pages, cache_pages, preferred_element_ty...  3.06 us
    dot_general x1, matrix products, fold_pages(): jnp.einsum('ps,phc->shc', onehot, factor[:, :, None] * page_acc, precisio...  2.69 us
  transfers between devices with their start and end apart: 9, of which 3 were waited for; matrix products, arithmetic and copies ran while one was open for 0% of the time, Pallas kernels for 0%

commit v1 on v0

v1 whole, which is shorter than its diff:
```python
import functools
import math

import jax
import jax.numpy as jnp
from jax import lax
from jax.experimental import pallas as pl
from jax.experimental.pallas import tpu as pltpu
from jax.sharding import PartitionSpec as P

LATENT = 512
SCALE = 192.0 ** (-0.5) * math.log2(math.e)
NEG = -1e30
KV_COPIES = 6
PIECES = 2
LAG = 2
MESH = pl.DeviceIdType.MESH


def kernel(
    n,
    counts_ref,
    tails_ref,
    slots_ref,
    latent_ref,
    q_hbm,
    kv_hbm,
    out_ref,
    q_v,
    kv_v,
    bias_v,
    score_v,
    weight_v,
    acc_v,
    inbox,
    part_v,
    cross,
    total_v,
    final,
    stat_out,
    stat_in,
    load_sem,
    stat_send,
    stat_recv,
    in_send,
    in_recv,
    cross_recv,
    fin_send,
    fin_recv,
):
    batch, rows, width = q_v.shape
    pages, page, _ = kv_hbm.shape[1:]
    tokens = pages * page
    slots = slots_ref.shape[1]
    me = lax.axis_index("ctx")
    half = n // 2
    left = me < half
    inward = jnp.where(left, me + 1, me - 1)
    outward = jnp.where(left, me - 1, me + 1)
    is_end = (me == 0) | (me == n - 1)
    is_mid = (me == half - 1) | (me == half)
    inner = jnp.logical_not(is_end)

    loads = [pltpu.make_async_copy(q_hbm.at[0], q_v, load_sem.at[KV_COPIES])]
    step = pages // KV_COPIES
    for i in range(KV_COPIES):
        loads.append(
            pltpu.make_async_copy(
                kv_hbm.at[0, pl.ds(i * step, step)],
                kv_v.at[pl.ds(i * step, step)],
                load_sem.at[i],
            )
        )
    for load in loads:
        load.start()

    barrier = pltpu.get_barrier_semaphore()

    @pl.loop(1, n)
    def _(off):
        pl.semaphore_signal(
            barrier, inc=1, device_id={"ctx": lax.rem(me + off, n)}, device_id_type=MESH
        )

    kv_v[pages] = jnp.zeros((page, width), jnp.bfloat16)
    kv_v[pages, 0:batch, :] = latent_ref[0]

    slot_id = me * pages + lax.broadcasted_iota(jnp.int32, (pages, slots), 0)
    rank = lax.broadcasted_iota(jnp.int32, (pages, slots), 1)
    match = slots_ref[...] == slot_id
    lane = lax.broadcasted_iota(jnp.int32, (pages, page), 1)
    lane_own = lax.broadcasted_iota(jnp.int32, (8, page), 1)
    begin = jnp.int32(0)
    for s in range(batch):
        count = counts_ref[0, s]
        length = (count - 1) * page + tails_ref[0, s]
        place = rank - begin
        inside = match & (place >= 0) & (place < count)
        limit = jnp.sum(
            jnp.where(inside, (length - place * page).astype(jnp.float32), 0.0),
            axis=1,
            keepdims=True,
        )
        bias_v[s, 0:pages, :] = jnp.where(lane.astype(jnp.float32) < limit, 0.0, NEG)
        own_here = (lane_own == s) & (me == 0)
        bias_v[s, pages : pages + 8, :] = jnp.where(own_here, 0.0, NEG)
        begin = begin + count

    loads[0].wait()
    queries = q_v[...].reshape(batch * rows, width)
    tops = [jnp.full((rows, page), NEG, jnp.float32) for _ in range(batch)]
    nt = (((1,), (1,)), ((), ()))
    for first in range(0, pages + 1, 2):
        if first < pages and first % step == 0:
            loads[1 + first // step].wait()
        many = min(2, pages + 1 - first)
        keys = kv_v[first : first + many].reshape(many * page, width)
        block = lax.dot_general(queries, keys, nt, preferred_element_type=jnp.float32)
        for s in range(batch):
            for j in range(many):
                at = first + j
                value = (
                    block[s * rows : (s + 1) * rows, j * page : (j + 1) * page] * SCALE
                    + bias_v[s, at : at + 1, :]
                )
                score_v[s, :, at * page : (at + 1) * page] = value
                tops[s] = jnp.maximum(tops[s], value)

    size = rows // PIECES

    def piece(k):
        return k // PIECES, pl.ds((k % PIECES) * size, size)

    def ship(source, target, send, recv, k, to):
        s, at = piece(k)
        return pltpu.make_async_remote_copy(
            src_ref=source.at[s, at],
            dst_ref=target.at[s, at],
            send_sem=send.at[k],
            recv_sem=recv.at[k],
            device_id={"ctx": to},
            device_id_type=MESH,
        )

    def stat_copy(s, to, origin, slot):
        return pltpu.make_async_remote_copy(
            src_ref=stat_out.at[s],
            dst_ref=stat_in.at[s, origin],
            send_sem=stat_send.at[s, slot],
            recv_sem=stat_recv.at[s, origin],
            device_id={"ctx": to},
            device_id_type=MESH,
        )

    def other(off):
        to = lax.rem(me + off, n)
        return to, (to > 0) & (to < n - 1)

    lane_row = lax.broadcasted_iota(jnp.int32, (rows, page), 1)
    for s in range(batch):
        top = jnp.max(tops[s], axis=1, keepdims=True)
        total = jnp.zeros((rows, page), jnp.float32)
        for at in range(pages + 1):
            cols = slice(at * page, (at + 1) * page)
            weight = jnp.exp2(score_v[s, :, cols] - top).astype(jnp.bfloat16)
            weight_v[s % 2, :, cols] = weight
            total = total + weight.astype(jnp.float32)
        total = jnp.sum(total, axis=1, keepdims=True)
        pair = jnp.where(lane_row == 0, top, total)
        square = jnp.concatenate([pair] * (page // rows), axis=0)
        tile = jnp.transpose(square)[0:8]
        stat_out[s] = tile
        stat_in[s, pl.ds(me, 1)] = tile[None]
        if s == 0:
            pl.semaphore_wait(barrier, n - 1)

        @pl.loop(1, n)
        def _(off):
            to, wanted = other(off)

            @pl.when(wanted)
            def _():
                stat_copy(s, to, me, off).start()

        values = kv_v[...].reshape(tokens + page, width)[:, :LATENT]
        acc_v[s] = jnp.dot(weight_v[s % 2], values, preferred_element_type=jnp.float32)

        @pl.when(is_end)
        def _():
            for k in range(s * PIECES, (s + 1) * PIECES):
                ship(acc_v, inbox, in_send, in_recv, k, inward).start()

    number = batch * PIECES
    from_end = (outward == 0) | (outward == n - 1)

    def factors(s):
        @pl.loop(1, n)
        def _(off):
            stat_copy(s, me, lax.rem(me + off, n), off).wait_recv()

        best = stat_in[s, 0]
        for j in range(1, n):
            best = jnp.maximum(best, stat_in[s, j])
        best = best[0:1]
        denom = jnp.zeros((1, page), jnp.float32)
        mine = jnp.zeros((1, page), jnp.float32)
        theirs = jnp.zeros((1, page), jnp.float32)
        for j in range(n):
            tile = stat_in[s, j]
            keep = jnp.exp2(tile[0:1] - best)
            denom = denom + keep * tile[1:2]
            mine = jnp.where(me == j, keep, mine)
            theirs = jnp.where(outward == j, keep, theirs)
        mine = mine / denom
        theirs = jnp.where(from_end, theirs / denom, 1.0)
        row = lax.broadcasted_iota(jnp.int32, (page, page), 0)
        turned = jnp.transpose(jnp.where(row == 0, mine, theirs))
        return turned[0:rows, 0:1], turned[0:rows, 1:2]

    @pl.when(inner)
    def _():
        scales = {}
        for k in range(number + LAG):
            if k < number:
                s, at = piece(k)
                if k % PIECES == 0:
                    scales[s] = factors(s)
                lo = (k % PIECES) * size
                mine, theirs = (f[lo : lo + size] for f in scales[s])
                ship(acc_v, inbox, in_send, in_recv, k, inward).wait_recv()
                part_v[s, at] = acc_v[s, at] * mine + inbox[s, at] * theirs

                @pl.when(is_mid)
                def _():
                    ship(part_v, cross, in_send, cross_recv, k, inward).start()

                @pl.when(jnp.logical_not(is_mid))
                def _():
                    ship(part_v, inbox, in_send, in_recv, k, inward).start()

            if k >= LAG:
                d = k - LAG
                s, at = piece(d)

                @pl.when(is_mid)
                def _():
                    ship(part_v, cross, in_send, cross_recv, d, inward).wait_recv()
                    total = part_v[s, at] + cross[s, at]
                    total_v[s, at] = total
                    ship(total_v, final, fin_send, fin_recv, d, outward).start()
                    out_ref[0, s, at] = total.astype(jnp.bfloat16)

                @pl.when(jnp.logical_not(is_mid))
                def _():
                    ship(final, final, fin_send, fin_recv, d, outward).wait_recv()
                    ship(final, final, fin_send, fin_recv, d, outward).start()
                    out_ref[0, s, at] = final[s, at].astype(jnp.bfloat16)

        for k in range(number):
            ship(total_v, final, fin_send, fin_recv, k, outward).wait_send()

    @pl.when(is_end)
    def _():
        for k in range(number):
            s, at = piece(k)
            ship(total_v, final, fin_send, fin_recv, k, inward).wait_recv()
            out_ref[0, s, at] = final[s, at].astype(jnp.bfloat16)

    for k in range(number):
        ship(part_v, inbox, in_send, in_recv, k, inward).wait_send()
    for s in range(batch):

        @pl.loop(1, n)
        def _(off):
            to, wanted = other(off)

            @pl.when(wanted)
            def _():
                stat_copy(s, to, me, off).wait_send()


def local(n, kv_cache, queries, new_latent, page_counts, page_tails, page_slots):
    _, pages, page, width = kv_cache.shape
    _, batch, rows, _ = queries.shape
    number = batch * PIECES
    block = (batch, rows, LATENT)
    vmem = pl.BlockSpec(memory_space=pltpu.VMEM)
    smem = pl.BlockSpec(memory_space=pltpu.SMEM)
    hbm = pl.BlockSpec(memory_space=pl.ANY)
    dma = pltpu.SemaphoreType.DMA
    return pl.pallas_call(
        functools.partial(kernel, n),
        out_shape=jax.ShapeDtypeStruct((1,) + block, jnp.bfloat16),
        in_specs=[smem, smem, vmem, vmem, hbm, hbm],
        out_specs=vmem,
        scratch_shapes=[
            pltpu.VMEM((batch, rows, width), jnp.bfloat16),
            pltpu.VMEM((pages + 1, page, width), jnp.bfloat16),
            pltpu.VMEM((batch, pages + 8, page), jnp.float32),
            pltpu.VMEM((batch, rows, (pages + 1) * page), jnp.float32),
            pltpu.VMEM((2, rows, (pages + 1) * page), jnp.bfloat16),
            pltpu.VMEM(block, jnp.float32),
            pltpu.VMEM(block, jnp.float32),
            pltpu.VMEM(block, jnp.float32),
            pltpu.VMEM(block, jnp.float32),
            pltpu.VMEM(block, jnp.float32),
            pltpu.VMEM(block, jnp.float32),
            pltpu.VMEM((batch, 8, page), jnp.float32),
            pltpu.VMEM((batch, n, 8, page), jnp.float32),
            dma((KV_COPIES + 1,)),
            dma((batch, n)),
            dma((batch, n)),
            dma((number,)),
            dma((number,)),
            dma((number,)),
            dma((number,)),
            dma((number,)),
        ],
        compiler_params=pltpu.CompilerParams(collective_id=0, has_side_effects=True),
    )(page_counts, page_tails, page_slots, new_latent, queries, kv_cache)


def solution(mesh):
    in_specs = (
        P(("groups", "rep"), "ctx", None, None),
        P(("groups", "rep"), None, "head", None),
        P(("groups", "rep"), None, None),
        P(("groups", "rep"), None),
        P(("groups", "rep"), None),
        P(("groups", "rep"), None),
    )
    out_specs = P(("groups", "rep"), None, "head", None)
    return jax.shard_map(
        functools.partial(local, mesh.shape["ctx"]),
        mesh=mesh,
        in_specs=in_specs,
        out_specs=out_specs,
        check_vma=False,
    )
```

time: 70.3 us -> 38.4 us (0.55)
  waiting for transfers between devices: 36.3 us -> 0 us
  Pallas kernels: 0 us -> 30.4 us
  starting transfers between devices: 10 us -> 0 us
  other arithmetic: 9.72 us -> 0 us
  matrix products: 9.49 us -> 0 us
  local copies, waits for them, and re-layouts: 4.24 us -> 7.73 us
    ppermute x9 -> x0, waiting for transfers between devices: 36.3 us -> none  [from_behind(): lax.ppermute(shard, axis, [(i, (i + by) % size) for i in range(size)])]
    pallas_call x0 -> x1, Pallas kernels: none -> 30.4 us  [local(): pl.pallas_call(functools.partial(kernel, n), out_shape=jax.ShapeDtypeStru...]
    ppermute x9 -> x0, starting transfers between devices: 10 us -> none  [from_behind(): lax.ppermute(shard, axis, [(i, (i + by) % size) for i in range(size)])]
    dot_general x5 -> x0, matrix products: 9.49 us -> none  [the longest x1 3.42 us: page_partials(): jnp.einsum('pht,ptc->phc', weights, cache_pages[:, :, :LATENT], preferred...]
    unnamed x13 -> x2, local copies, waits for them, and re-layouts: 1.03 us -> 7.73 us
    sub x1 -> x0, other arithmetic: 4.99 us -> none  [page_layout(): limit = jnp.take(lengths, sequence_of) - page_number * page_width]
    gather x3 -> x0, local copies, waits for them, and re-layouts: 2.18 us -> none  [the longest x1 0.92 us: local(): query_pages = jnp.take(query_block, sequence_of, axis=0)]
    reduce_sum x3 -> x0, other arithmetic: 1.45 us -> none  [the longest x1 0.83 us: page_layout(): page_rank = jnp.sum(jnp.where(matches, pack_rank[:, None], 0), axis=0)]
  transfers between devices with their start and end apart: 9 -> 0, of which waited for: 3 -> 0; matrix products, arithmetic and copies ran while one was open for 0% -> 0% of each run, Pallas kernels for 0% -> 0%
where the time goes in v1:
time: 38.4 us; the launch traced here: 38.1 us
  Pallas kernels  30.4 us (79%)
  local copies, waits for them, and re-layouts  7.73 us (20%)
    pallas_call x1, Pallas kernels, local(): pl.pallas_call(functools.partial(kernel, n), out_shape=jax.ShapeDtypeStru...  30.4 us
    unnamed x2, local copies, waits for them, and re-layouts  7.73 us

profile of v1, /device:TPU:0, one launch (start us, length us, event | category | flops | bytes accessed | tf_op | source)
XLA Modules:
  0.0 38.1 jit_solution(1271011964111492471)
XLA Ops:
  0.0 6.1 %copy.7.kv_hbm = bf16[1,24,128,576]{3,2,1,0:T(8,128)(2,1)} copy(bf16[1,24,128,576]{2,3,1,0:T(8,128)(2,1)} %param.6) | data formatting | bytes 7077888 | tf_op args[0]
  6.1 30.4 %shard_map.64 = bf16[1,4,64,512]{3,2,1,0:T(8,128)(2,1)} custom-call(s32[1,4]{1,0:T(1,128)} %counts_ref.1, s32[1,4]{1,0:T(1,128)} %tails_ref.1, s32[1,96]{1,0:T(1,128)} %slots_ref.1, bf16[1,4,576]{2,1,0:T(4,128)(2,1)} %latent_ref.1, bf16[1,4,64,576]{3,2,1,0:T(8,128)(2,1)} %q_hbm.1, bf16[1,24,128,576]{3,2,1,0:T(8,128)(2,1)} %copy.7.kv_hbm), custom_call_target="tpu_custom_call" | custom-call | tf_op jit(solution)/shard_map/pallas_call | solution.py:291
  36.5 1.7 %copy.9 = bf16[1,4,64,512]{3,2,1,0:T(8,128)(2,1)} copy(bf16[1,4,64,512]{3,2,1,0:T(8,128)(2,1)} %shard_map.64) | data formatting | bytes 524288

commit v2 on v1

--- a/solution.py
+++ b/solution.py
@@ -11,9 +11,8 @@
 LATENT = 512
 SCALE = 192.0 ** (-0.5) * math.log2(math.e)
 NEG = -1e30
-KV_COPIES = 6
-PIECES = 2
-LAG = 2
+PIECES = 4
+LAG = 6
 MESH = pl.DeviceIdType.MESH
 
 
@@ -28,6 +27,7 @@
     out_ref,
     q_v,
     kv_v,
+    own_v,
     bias_v,
     score_v,
     weight_v,
@@ -49,7 +49,7 @@
     fin_recv,
 ):
     batch, rows, width = q_v.shape
-    pages, page, _ = kv_hbm.shape[1:]
+    pages, _, page = kv_hbm.shape[1:]
     tokens = pages * page
     slots = slots_ref.shape[1]
     me = lax.axis_index("ctx")
@@ -61,13 +61,12 @@
     is_mid = (me == half - 1) | (me == half)
     inner = jnp.logical_not(is_end)
 
-    loads = [pltpu.make_async_copy(q_hbm.at[0], q_v, load_sem.at[KV_COPIES])]
-    step = pages // KV_COPIES
-    for i in range(KV_COPIES):
+    loads = [pltpu.make_async_copy(q_hbm.at[0], q_v, load_sem.at[pages])]
+    for i in range(pages):
         loads.append(
             pltpu.make_async_copy(
-                kv_hbm.at[0, pl.ds(i * step, step)],
-                kv_v.at[pl.ds(i * step, step)],
+                kv_hbm.at[0, i],
+                kv_v.at[:, pl.ds(i * page, page)],
                 load_sem.at[i],
             )
         )
@@ -82,8 +81,8 @@
             barrier, inc=1, device_id={"ctx": lax.rem(me + off, n)}, device_id_type=MESH
         )
 
-    kv_v[pages] = jnp.zeros((page, width), jnp.bfloat16)
-    kv_v[pages, 0:batch, :] = latent_ref[0]
+    own_v[...] = jnp.zeros((page, width), jnp.bfloat16)
+    own_v[0:batch, :] = latent_ref[0]
 
     slot_id = me * pages + lax.broadcasted_iota(jnp.int32, (pages, slots), 0)
     rank = lax.broadcasted_iota(jnp.int32, (pages, slots), 1)
@@ -110,12 +109,17 @@
     queries = q_v[...].reshape(batch * rows, width)
     tops = [jnp.full((rows, page), NEG, jnp.float32) for _ in range(batch)]
     nt = (((1,), (1,)), ((), ()))
-    for first in range(0, pages + 1, 2):
-        if first < pages and first % step == 0:
-            loads[1 + first // step].wait()
-        many = min(2, pages + 1 - first)
-        keys = kv_v[first : first + many].reshape(many * page, width)
-        block = lax.dot_general(queries, keys, nt, preferred_element_type=jnp.float32)
+    for first in [*range(0, pages, 2), pages]:
+        many = min(2, pages - first) or 1
+        if first < pages:
+            for j in range(many):
+                loads[1 + first + j].wait()
+            keys = kv_v[:, first * page : (first + many) * page]
+            block = jnp.dot(queries, keys, preferred_element_type=jnp.float32)
+        else:
+            block = lax.dot_general(
+                queries, own_v[...], nt, preferred_element_type=jnp.float32
+            )
         for s in range(batch):
             for j in range(many):
                 at = first + j
@@ -126,7 +130,8 @@
                 score_v[s, :, at * page : (at + 1) * page] = value
                 tops[s] = jnp.maximum(tops[s], value)
 
-    size = rows // PIECES
+    size = batch * rows // PIECES
+    wide = out_ref.shape[3] // page
 
     def piece(k):
         return k // PIECES, pl.ds((k % PIECES) * size, size)
@@ -163,7 +168,7 @@
         for at in range(pages + 1):
             cols = slice(at * page, (at + 1) * page)
             weight = jnp.exp2(score_v[s, :, cols] - top).astype(jnp.bfloat16)
-            weight_v[s % 2, :, cols] = weight
+            weight_v[s * rows : (s + 1) * rows, cols] = weight
             total = total + weight.astype(jnp.float32)
         total = jnp.sum(total, axis=1, keepdims=True)
         pair = jnp.where(lane_row == 0, top, total)
@@ -182,15 +187,33 @@
             def _():
                 stat_copy(s, to, me, off).start()
 
-        values = kv_v[...].reshape(tokens + page, width)[:, :LATENT]
-        acc_v[s] = jnp.dot(weight_v[s % 2], values, preferred_element_type=jnp.float32)
+    group = 2
+    for j in range(0, wide, group):
+        span = slice(j * page, (j + group) * page)
+        block = lax.dot_general(
+            weight_v[:, 0:tokens], kv_v[span, :], nt, preferred_element_type=jnp.float32
+        ) + jnp.dot(
+            weight_v[:, tokens:], own_v[:, span], preferred_element_type=jnp.float32
+        )
+        for i in range(group):
+            acc_v[j + i] = block[:, i * page : (i + 1) * page]
 
         @pl.when(is_end)
         def _():
-            for k in range(s * PIECES, (s + 1) * PIECES):
+            for k in range(j * PIECES, (j + group) * PIECES):
                 ship(acc_v, inbox, in_send, in_recv, k, inward).start()
 
-    number = batch * PIECES
+    def emit(k, value):
+        j = k // PIECES
+        first = (k % PIECES) * size
+        value = value.astype(jnp.bfloat16)
+        for lo in range(0, size, min(size, rows)):
+            s, r = divmod(first + lo, rows)
+            out_ref[0, s, r : r + min(size, rows), j * page : (j + 1) * page] = value[
+                lo : lo + min(size, rows)
+            ]
+
+    number = wide * PIECES
     from_end = (outward == 0) | (outward == n - 1)
 
     def factors(s):
@@ -219,14 +242,13 @@
 
     @pl.when(inner)
     def _():
-        scales = {}
+        pairs = [factors(s) for s in range(batch)]
+        scales = [jnp.concatenate(f, axis=0) for f in zip(*pairs)]
         for k in range(number + LAG):
             if k < number:
                 s, at = piece(k)
-                if k % PIECES == 0:
-                    scales[s] = factors(s)
                 lo = (k % PIECES) * size
-                mine, theirs = (f[lo : lo + size] for f in scales[s])
+                mine, theirs = (f[lo : lo + size] for f in scales)
                 ship(acc_v, inbox, in_send, in_recv, k, inward).wait_recv()
                 part_v[s, at] = acc_v[s, at] * mine + inbox[s, at] * theirs
 
@@ -248,13 +270,13 @@
                     total = part_v[s, at] + cross[s, at]
                     total_v[s, at] = total
                     ship(total_v, final, fin_send, fin_recv, d, outward).start()
-                    out_ref[0, s, at] = total.astype(jnp.bfloat16)
+                    emit(d, total)
 
                 @pl.when(jnp.logical_not(is_mid))
                 def _():
                     ship(final, final, fin_send, fin_recv, d, outward).wait_recv()
                     ship(final, final, fin_send, fin_recv, d, outward).start()
-                    out_ref[0, s, at] = final[s, at].astype(jnp.bfloat16)
+                    emit(d, final[s, at])
 
         for k in range(number):
             ship(total_v, final, fin_send, fin_recv, k, outward).wait_send()
@@ -264,7 +286,7 @@
         for k in range(number):
             s, at = piece(k)
             ship(total_v, final, fin_send, fin_recv, k, inward).wait_recv()
-            out_ref[0, s, at] = final[s, at].astype(jnp.bfloat16)
+            emit(k, final[s, at])
 
     for k in range(number):
         ship(part_v, inbox, in_send, in_recv, k, inward).wait_send()
@@ -282,23 +304,24 @@
 def local(n, kv_cache, queries, new_latent, page_counts, page_tails, page_slots):
     _, pages, page, width = kv_cache.shape
     _, batch, rows, _ = queries.shape
-    number = batch * PIECES
-    block = (batch, rows, LATENT)
+    number = LATENT // page * PIECES
+    block = (LATENT // page, batch * rows, page)
     vmem = pl.BlockSpec(memory_space=pltpu.VMEM)
     smem = pl.BlockSpec(memory_space=pltpu.SMEM)
-    hbm = pl.BlockSpec(memory_space=pl.ANY)
+    hbm = pl.BlockSpec(memory_space=pltpu.HBM)
     dma = pltpu.SemaphoreType.DMA
     return pl.pallas_call(
         functools.partial(kernel, n),
-        out_shape=jax.ShapeDtypeStruct((1,) + block, jnp.bfloat16),
+        out_shape=jax.ShapeDtypeStruct((1, batch, rows, LATENT), jnp.bfloat16),
         in_specs=[smem, smem, vmem, vmem, hbm, hbm],
         out_specs=vmem,
         scratch_shapes=[
             pltpu.VMEM((batch, rows, width), jnp.bfloat16),
-            pltpu.VMEM((pages + 1, page, width), jnp.bfloat16),
+            pltpu.VMEM((width, pages * page), jnp.bfloat16),
+            pltpu.VMEM((page, width), jnp.bfloat16),
             pltpu.VMEM((batch, pages + 8, page), jnp.float32),
             pltpu.VMEM((batch, rows, (pages + 1) * page), jnp.float32),
-            pltpu.VMEM((2, rows, (pages + 1) * page), jnp.bfloat16),
+            pltpu.VMEM((batch * rows, (pages + 1) * page), jnp.bfloat16),
             pltpu.VMEM(block, jnp.float32),
             pltpu.VMEM(block, jnp.float32),
             pltpu.VMEM(block, jnp.float32),
@@ -307,7 +330,7 @@
             pltpu.VMEM(block, jnp.float32),
             pltpu.VMEM((batch, 8, page), jnp.float32),
             pltpu.VMEM((batch, n, 8, page), jnp.float32),
-            dma((KV_COPIES + 1,)),
+            dma((pages + 1,)),
             dma((batch, n)),
             dma((batch, n)),
             dma((number,)),
@@ -316,8 +339,10 @@
             dma((number,)),
             dma((number,)),
         ],
-        compiler_params=pltpu.CompilerParams(collective_id=0, has_side_effects=True),
-    )(page_counts, page_tails, page_slots, new_latent, queries, kv_cache)
+        compiler_params=pltpu.CompilerParams(
+            collective_id=0, has_side_effects=True
+        ),
+    )(page_counts, page_tails, page_slots, new_latent, queries, jnp.swapaxes(kv_cache, 2, 3))
 
 
 def solution(mesh):

time: 38.4 us -> 34.5 us (0.90)
  local copies, waits for them, and re-layouts: 7.73 us -> 1.67 us
  Pallas kernels: 30.4 us -> 32.6 us
    unnamed x2 -> x1, local copies, waits for them, and re-layouts: 7.73 us -> 1.67 us
    pallas_call x1, Pallas kernels: 30.4 us -> 32.6 us  [local(): pl.pallas_call(functools.partial(kernel, n), out_shape=jax.ShapeDtypeStru...]
where the time goes in v2:
time: 34.5 us; the launch traced here: 34.3 us
  Pallas kernels  32.6 us (94%)
  local copies, waits for them, and re-layouts  1.67 us (5%)
    pallas_call x1, Pallas kernels, local(): pl.pallas_call(functools.partial(kernel, n), out_shape=jax.ShapeDtypeStru...  32.6 us
    unnamed x1, local copies, waits for them, and re-layouts  1.67 us

profile of v2, /device:TPU:0, one launch (start us, length us, event | category | flops | bytes accessed | tf_op | source)
XLA Modules:
  0.0 34.3 jit_solution(7368985828991238047)
XLA Ops:
  0.0 32.6 %shard_map.64 = bf16[1,4,64,512]{3,2,1,0:T(8,128)(2,1)} custom-call(s32[1,4]{1,0:T(1,128)} %counts_ref.1, s32[1,4]{1,0:T(1,128)} %tails_ref.1, s32[1,96]{1,0:T(1,128)} %slots_ref.1, bf16[1,4,576]{2,1,0:T(4,128)(2,1)} %latent_ref.1, bf16[1,4,64,576]{3,2,1,0:T(8,128)(2,1)} %q_hbm.1, bf16[1,24,576,128]{3,2,1,0:T(8,128)(2,1)} %bitcast.1), custom_call_target="tpu_custom_call" | custom-call | tf_op jit(solution)/shard_map/pallas_call | solution.py:313
  32.6 1.7 %copy.8 = bf16[1,4,64,512]{3,2,1,0:T(8,128)(2,1)} copy(bf16[1,4,64,512]{3,2,1,0:T(8,128)(2,1)} %shard_map.64) | data formatting | bytes 524288
